TPU v7x, 16 devices: a 4x2x1 block of a 4x4x8 slice. The times are simulated.
16 devices in a mesh: dp: 4 (over y, z, core), ep: 4 (over x).
Axes of the slice: x: 4, y: 2, z: 1, core: 2. Of those that a mesh axis runs over, the one named last changes fastest.
The devices are a block of a 4x4x8 slice.
Arguments:
- x: bfloat16 [4, 4, 256, 7168], P('dp', 'ep'), parts along dimension 0
- expert: int32 [4, 4, 256, 2], P('dp', 'ep'), parts along dimension 0
- slot: int32 [4, 4, 256, 2], P('dp', 'ep'), parts along dimension 0
- gate: float32 [4, 4, 256, 2], P('dp', 'ep'), parts along dimension 0
- w_gate: bfloat16 [8, 7168, 4864], P('ep')
- w_up: bfloat16 [8, 7168, 4864], P('ep')
- w_down: bfloat16 [8, 4864, 7168], P('ep')
Outputs:
- y: bfloat16 [4, 4, 256, 7168], P('dp', 'ep'), parts along dimension 0
There are 4 independent parts. A program takes and returns all parts, laid end to end along the dimension named above; an argument that names none is the same for every part.
All inputs are finite; a program needn't handle non-finite values.
Results may differ from a plain program's by a relative error of at most 0.009.
Values are sent between devices in bfloat16 or wider.
A program may use at most 768 MiB of HBM per device.

v0:
```python
import jax
import jax.numpy as jnp
from jax import lax
from jax.sharding import NamedSharding, PartitionSpec as P


def einsum(form, a, b):
    return jnp.einsum(form, a.astype(jnp.float32), b.astype(jnp.float32))


def solution(mesh):
    def placed(v, *spec):
        return lax.with_sharding_constraint(v, NamedSharding(mesh, P(*spec)))

    def step(x, expert, slot, gate, w_gate, w_up, w_down):
        experts, (tokens, top) = w_gate.shape[0], expert.shape[2:]
        slots = 5 * tokens * top // (4 * experts)
        to_expert = jax.nn.one_hot(expert, experts, dtype=jnp.bfloat16)
        to_slot = jax.nn.one_hot(slot, slots, dtype=jnp.bfloat16)
        weighted = to_expert * gate[..., None].astype(jnp.bfloat16)
        dispatch = einsum("abtke,abtkc->abtec", to_expert, to_slot).astype(jnp.bfloat16)
        combine = einsum("abtke,abtkc->abtec", weighted, to_slot).astype(jnp.bfloat16)
        z = einsum("abtec,abtd->aebcd", dispatch, x).astype(jnp.bfloat16)
        z = placed(z, "dp", None, "ep", None, None)
        z = placed(z, "dp", "ep", None, None, None)
        h = jax.nn.silu(einsum("aebcd,edf->aebcf", z, w_gate))
        h = (h * einsum("aebcd,edf->aebcf", z, w_up)).astype(jnp.bfloat16)
        out = einsum("aebcf,efd->aebcd", h, w_down).astype(jnp.bfloat16)
        out = placed(out, "dp", "ep", None, None, None)
        out = placed(out, "dp", None, "ep", None, None)
        y = einsum("abtec,aebcd->abtd", combine, out)
        return y.astype(jnp.bfloat16)

    return step
```

profile of v0, /device:TPU:112, one launch (start us, length us, event | category | flops | bytes accessed | tf_op | source)
XLA Modules:
  0.0 421.8 jit_solution(13997407621514711572)
XLA Ops:
  0.0 0.8 copy.11
  0.8 0.0 copy-start
  0.8 0.8 copy.9
  1.7 0.0 copy-start.2
  1.7 1.8 convolution_convert_fusion.1
  3.4 4.6 %convolution_convert_fusion = bf16[8,80,7168]{2,1,0:T(8,128)(2,1)S(1)} fusion(bf16[1,1,256,7168]{3,2,1,0:T(8,128)(2,1)} %param.3, bf16[256,8,80]{2,1,0:T(8,128)(2,1)S(1)} %convolution_convert_fusion.1), kind=kOutput, calls=%fused_computation.14 | convolution fusion | flops 2353397760 | bytes 13172736 | tf_op jit(solution)/abtec,abtd->aebcd/dot_general | solution.py:8
  8.1 107.4 %all-to-all.4 = bf16[1,4,2,1,80,7168]{5,4,2,3,0,1:T(8,128)(2,1)} all-to-all(bf16[1,4,2,1,80,7168]{5,4,2,3,0,1:T(8,128)(2,1)S(1)} %bitcast.99), channel_id=1, replica_groups=mesh['dp'=4,'ep'=4] {'ep'}, dimensions={1} | all-to-all | bytes 18350080 | tf_op jit(solution)/sharding_constraint;jit(solution)/sharding_constraint | solution.py:13
  115.4 0.0 copy-done
  115.4 0.0 copy-done.2
  115.4 59.3 %fusion.2 = f32[2,4,80,4864]{3,2,1,0:T(8,128)} fusion(bf16[2,7168,4864]{2,1,0:T(8,128)(2,1)} %param.5, bf16[1,4,2,1,80,7168]{5,4,2,3,0,1:T(8,128)(2,1)} %all-to-all.4), kind=kOutput, calls=%fused_computation.2 | convolution fusion | flops 44627394560 | bytes 161087488 | tf_op jit(solution)/aebcd,edf->aebcf/dot_general | solution.py:8
  174.8 59.2 %fusion.4 = f32[2,4,80,4864]{3,2,1,0:T(8,128)} fusion(bf16[2,7168,4864]{2,1,0:T(8,128)(2,1)} %param.4, bf16[1,4,2,1,80,7168]{5,4,2,3,0,1:T(8,128)(2,1)} %all-to-all.4), kind=kOutput, calls=%fused_computation.4 | convolution fusion | flops 44627394560 | bytes 161087488 | tf_op jit(solution)/aebcd,edf->aebcf/dot_general | solution.py:8
  234.0 64.4 %fusion.13 = bf16[1,2,4,1,80,7168]{5,4,2,1,3,0:T(8,128)(2,1)} fusion(bf16[2,4864,7168]{2,1,0:T(8,128)(2,1)} %param.6, f32[2,4,80,4864]{3,2,1,0:T(8,128)} %fusion.2, f32[2,4,80,4864]{3,2,1,0:T(8,128)} %fusion.4), kind=kOutput, calls=%fused_computation.15 | convolution fusion | flops 44650659840 | bytes 173539328 | tf_op jit(solution)/aebcf,efd->aebcd/dot_general | solution.py:8
  298.3 7.7 %copy.15 = bf16[1,2,4,1,80,7168]{5,4,1,3,0,2:T(8,128)(2,1)} copy(bf16[1,2,4,1,80,7168]{5,4,2,1,3,0:T(8,128)(2,1)} %fusion.13) | data formatting | bytes 18350080 | tf_op jit(solution)/sharding_constraint;jit(solution)/sharding_constraint | solution.py:13
  306.1 0.0 copy-start.4
  306.1 0.0 copy-start.1
  306.1 0.0 copy-start.3
  306.1 6.0 %all-to-all-start.1 = ((bf16[1,2,4,1,80,7168]{5,4,1,3,0,2:T(8,128)(2,1)}), bf16[1,2,4,1,80,7168]{5,4,1,3,0,2:T(8,128)(2,1)}, u32[]{:S(2)}, u32[]{:S(2)}) async-start(bf16[1,2,4,1,80,7168]{5,4,1,3,0,2:T(8,128)(2,1)} %copy.15), calls=%async_computation.1 | async-start | bytes 18350080 | tf_op jit(solution)/sharding_constraint;jit(solution)/sharding_constraint | solution.py:13
  312.1 0.0 copy-done.4
  312.1 0.1 copy.10
  312.2 0.0 copy-done.1
  312.2 0.0 copy-done.3
  312.2 2.2 convolution_convert_fusion.2
  314.5 98.8 %all-to-all-done.1 = bf16[1,2,4,1,80,7168]{5,4,1,3,0,2:T(8,128)(2,1)} async-done(((bf16[1,2,4,1,80,7168]{5,4,1,3,0,2:T(8,128)(2,1)}), bf16[1,2,4,1,80,7168]{5,4,1,3,0,2:T(8,128)(2,1)}, u32[]{:S(2)}, u32[]{:S(2)}) %all-to-all-start.1) | async-done | bytes 9175072 | tf_op jit(solution)/sharding_constraint;jit(solution)/sharding_constraint | solution.py:13
  413.2 8.5 %fusion.19 = bf16[1,1,256,7168]{3,2,1,0:T(8,128)(2,1)} fusion(bf16[8,80,7168]{2,1,0:T(8,128)(2,1)} %bitcast.25, bf16[256,8,80]{2,1,0:T(8,128)(2,1)S(1)} %convolution_convert_fusion.2), kind=kOutput, calls=%fused_computation.20 | convolution fusion | flops 2350645248 | bytes 13172736 | tf_op jit(solution)/abtec,aebcd->abtd/dot_general | solution.py:8
  (1 shorter events, 0.0 us)
Async XLA Ops:
  0.8 114.6 %copy-start = (s32[256,2]{1,0:T(8,128)}, s32[256,2]{1,0:T(8,128)S(1)}, u32[]{:S(2)}) copy-start(s32[256,2]{1,0:T(8,128)S(1)} %copy.11) | copy-start | bytes 6148
  1.7 113.8 %copy-start.2 = (s32[256,2]{1,0:T(8,128)}, s32[256,2]{1,0:T(8,128)S(1)}, u32[]{:S(2)}) copy-start(s32[256,2]{1,0:T(8,128)S(1)} %copy.9) | copy-start | bytes 6148
  306.1 6.0 %copy-start.4 = (f32[1,1,256,2]{2,3,1,0:T(2,128)S(1)}, f32[1,1,256,2]{2,3,1,0:T(2,128)}, u32[]{:S(2)}) copy-start(f32[1,1,256,2]{2,3,1,0:T(2,128)} %param.1) | copy-start | bytes 6148
  306.1 6.2 %copy-start.1 = (s32[256,2]{1,0:T(8,128)S(1)}, s32[256,2]{1,0:T(8,128)}, u32[]{:S(2)}) copy-start(s32[256,2]{1,0:T(8,128)} %copy-done) | copy-start | bytes 6148
  306.1 6.2 %copy-start.3 = (s32[256,2]{1,0:T(8,128)S(1)}, s32[256,2]{1,0:T(8,128)}, u32[]{:S(2)}) copy-start(s32[256,2]{1,0:T(8,128)} %copy-done.2) | copy-start | bytes 6148
  306.1 107.2 %all-to-all-start.1 = ((bf16[1,2,4,1,80,7168]{5,4,1,3,0,2:T(8,128)(2,1)}), bf16[1,2,4,1,80,7168]{5,4,1,3,0,2:T(8,128)(2,1)}, u32[]{:S(2)}, u32[]{:S(2)}) async-start(bf16[1,2,4,1,80,7168]{5,4,1,3,0,2:T(8,128)(2,1)} %copy.15), calls=%async_computation.1 | async-start | bytes 18350080 | tf_op jit(solution)/sharding_constraint;jit(solution)/sharding_constraint | solution.py:13
where the time goes:
time: 422 us
  matrix products  200 us (47%)
  blocking collectives  107 us (25%)
  waiting for transfers between devices  98.8 us (23%)
  local copies, waits for them, and re-layouts  9.55 us (2%)
  starting transfers between devices  5.98 us (1%)
    dot_general x7, matrix products, einsum(): return jnp.einsum(form, a.astype(jnp.float32), b.astype(jnp.float32))  200 us
    another operation x1, blocking collectives, placed(): return lax.with_sharding_constraint(v, NamedSharding(mesh, P(*spec)))  107 us
    another operation x1, waiting for transfers between devices, placed(): return lax.with_sharding_constraint(v, NamedSharding(mesh, P(*spec)))  98.8 us
  transfers between devices with their start and end apart: 1, of which 1 were waited for; matrix products, arithmetic and copies ran while one was open for 1% of the time, Pallas kernels for 0%

commit v1 on v0

v1 whole, which is shorter than its diff:
```python
import functools

import jax
import jax.numpy as jnp
from jax import lax
from jax.experimental import pallas as pl
from jax.experimental.pallas import tpu as pltpu
from jax.sharding import PartitionSpec as P

F32, BF16 = jnp.float32, jnp.bfloat16
CHUNK = 1024
KC = 512
NC = 256
TN = 256
DOWN = 4


def kernel(
    n, slots, x_hbm, expert_ref, slot_ref, gate_ref, wg_hbm, wu_hbm, wd_hbm, y_hbm,
    x_v, z, stage, back, acc_g, acc_u, h, w_a, w_b, w_c, w_d, wd_v, y_v, sel, comb_l, comb_r,
    x_sem, w_sem, wd_sem, y_sem, d_send, d_recv, c_send, c_recv,
):
    per, depth, ff = wg_hbm.shape
    tokens = x_hbm.shape[0]
    rows = n * slots
    chunks, steps, outs = depth // CHUNK, depth // KC, depth // NC
    per_chunk, outs_chunk = CHUNK // KC, CHUNK // NC
    lo = w_a.shape[1]
    me = lax.axis_index("ep")

    def peer(r):
        return {"ep": lax.rem(me + r, n)}

    def at(i, size):
        return pl.ds(pl.multiple_of(i * size, size), size)

    def x_copy(k):
        return pltpu.make_async_copy(x_hbm.at[:, at(k, CHUNK)], x_v.at[:, at(k, CHUNK)], x_sem.at[k])

    units = (
        (wg_hbm, w_a, acc_g, 0, lo), (wg_hbm, w_b, acc_g, lo, ff - lo),
        (wu_hbm, w_c, acc_u, 0, lo), (wu_hbm, w_d, acc_u, lo, ff - lo),
    )

    def w_copy(u, t):
        src, dst, _, off, width = units[u]
        return pltpu.make_async_copy(
            src.at[lax.div(t, steps), at(lax.rem(t, steps), KC), pl.ds(off, width)], dst, w_sem.at[u]
        )

    def wd_copy(t):
        b = lax.rem(t, DOWN)
        return pltpu.make_async_copy(
            wd_hbm.at[lax.div(t, outs), :, at(lax.rem(t, outs), NC)], wd_v.at[b], wd_sem.at[b]
        )

    def d_copy(e, k, r):
        return pltpu.make_async_remote_copy(
            src_ref=stage.at[pl.ds((r - 1) * slots, slots), at(k, CHUNK)],
            dst_ref=z.at[e, pl.ds(r * slots, slots), at(k, CHUNK)],
            send_sem=d_send.at[k, r - 1], recv_sem=d_recv.at[e, k, r - 1],
            device_id=peer(r), device_id_type=pl.DeviceIdType.MESH,
        )

    def c_copy(e, k, r):
        return pltpu.make_async_remote_copy(
            src_ref=z.at[e, pl.ds(r * slots, slots), at(k, CHUNK)],
            dst_ref=back.at[e, pl.ds((r - 1) * slots, slots), at(k, CHUNK)],
            send_sem=c_send.at[e, k, r - 1], recv_sem=c_recv.at[e, k, r - 1],
            device_id=peer(n - r), device_id_type=pl.DeviceIdType.MESH,
        )

    far_first = (2, 1, 3)

    for k in range(chunks):
        x_copy(k).start()
    for u in range(4):
        w_copy(u, 0).start()
    for t in range(DOWN):
        wd_copy(t).start()
    barrier = pltpu.get_barrier_semaphore()
    for r in range(1, n):
        pl.semaphore_signal(barrier, inc=1, device_id=peer(r), device_id_type=pl.DeviceIdType.MESH)

    ex, sl = expert_ref[...], slot_ref[...]
    owner = lax.shift_right_logical(ex, per.bit_length() - 1)
    place = lax.bitwise_and(owner - me + n, n - 1) * slots + sl
    local = lax.bitwise_and(ex, per - 1)
    gates = gate_ref[...].astype(BF16).astype(F32)
    for e in range(per):
        row = jnp.where(jnp.logical_and(local == e, sl < slots), place, -1)
        lane = lax.broadcasted_iota(jnp.int32, (tokens, rows), 1)
        hit = [row[:, j:j + 1] == lane for j in range(row.shape[1])]
        one = sum(jnp.where(m, 1.0, 0.0) for m in hit)
        sel[e] = one.T.astype(BF16)
        lane = lax.broadcasted_iota(jnp.int32, (tokens, slots), 1)
        comb_l[e] = sum(
            jnp.where(row[:, j:j + 1] == lane, gates[:, j:j + 1], 0.0) for j in range(row.shape[1])
        ).astype(BF16)
        lane = lax.broadcasted_iota(jnp.int32, (tokens, rows - slots), 1) + slots
        comb_r[e] = sum(
            jnp.where(row[:, j:j + 1] == lane, gates[:, j:j + 1], 0.0) for j in range(row.shape[1])
        ).astype(BF16)

    def gather(e, k):
        for i in range(CHUNK // TN):
            cols = pl.ds(pl.multiple_of(k * CHUNK + i * TN, TN), TN)
            part = jnp.dot(sel[e], x_v[:, cols], preferred_element_type=F32).astype(BF16)
            z[e, :slots, cols] = part[:slots]
            stage[:, cols] = part[slots:]

    def send(e, k):
        for r in far_first:
            d_copy(e, k, r).start()

    pl.semaphore_wait(barrier, n - 1)
    x_copy(0).wait()
    gather(0, 0)

    @pl.loop(1, chunks)
    def _(k):
        x_copy(k).wait()
        gather(0, k)
        send(0, k - 1)

    def clear(i, c):
        acc_g[:, at(i, TN)] = jnp.zeros((rows, TN), F32)
        acc_u[:, at(i, TN)] = jnp.zeros((rows, TN), F32)
        return c

    lax.fori_loop(0, ff // TN, clear, 0)
    send(0, chunks - 1)

    def again(k):
        for r in far_first:
            d_copy(0, k, r).wait_send()
        gather(1, k)

    for e in range(per):
        @pl.loop(0, steps)
        def _(c):
            @pl.when(lax.rem(c, per_chunk) == 0)
            def _():
                k = lax.div(c, per_chunk)
                for r in far_first:
                    d_copy(e, k, r).wait_recv()
                if e == 0:
                    @pl.when(k >= 1)
                    def _():
                        again(k - 1)
            cols = at(c, KC)
            t = e * steps + c
            for u, (_, buf, acc, off, width) in enumerate(units):
                w_copy(u, t).wait()
                for i in range(width // TN):
                    here = pl.ds(off + i * TN, TN)
                    acc[:, here] += jnp.dot(
                        z[e, :, cols], buf[:, pl.ds(i * TN, TN)], preferred_element_type=F32
                    )

                @pl.when(t + 1 < per * steps)
                def _():
                    w_copy(u, t + 1).start()
            if e == 0:
                @pl.when(jnp.logical_and(lax.rem(c, per_chunk) == 0, c >= per_chunk))
                def _():
                    send(1, lax.div(c, per_chunk) - 1)

        if e == 0:
            again(chunks - 1)

        def act(i, c):
            cols = at(i, TN)
            h[:, cols] = (jax.nn.silu(acc_g[:, cols]) * acc_u[:, cols]).astype(BF16)
            if e + 1 < per:
                acc_g[:, cols] = jnp.zeros((rows, TN), F32)
                acc_u[:, cols] = jnp.zeros((rows, TN), F32)
            return c

        lax.fori_loop(0, ff // TN, act, 0)
        if e == 0:
            send(1, chunks - 1)

        @pl.loop(0, outs // 2)
        def _(j2):
            for i in range(2):
                j = 2 * j2 + i
                t = e * outs + j
                wd_copy(t).wait()
                part = jnp.dot(h[...], wd_v[lax.rem(t, DOWN)], preferred_element_type=F32)
                z[e, :, at(j, NC)] = part.astype(BF16)

                @pl.when(t + DOWN < per * outs)
                def _():
                    wd_copy(t + DOWN).start()

            j = 2 * j2
            @pl.when(jnp.logical_and(lax.rem(j, outs_chunk) == 0, j > 0))
            def _():
                for r in far_first:
                    c_copy(e, lax.div(j, outs_chunk) - 1, r).start()

        if e + 1 < per:
            for r in far_first:
                c_copy(e, chunks - 1, r).start()

    def y_copy(k):
        b = lax.rem(k, 2)
        return pltpu.make_async_copy(y_v.at[b], y_hbm.at[:, at(k, CHUNK)], y_sem.at[b])

    def finish(k):
        for e in range(per):
            for r in far_first:
                c_copy(e, k, r).wait_recv()

        @pl.when(k >= 2)
        def _():
            y_copy(k - 2).wait()
        for i in range(CHUNK // TN):
            cols = pl.ds(pl.multiple_of(k * CHUNK + i * TN, TN), TN)
            total = 0.0
            for e in range(per):
                total += jnp.dot(comb_l[e], z[e, :slots, cols], preferred_element_type=F32)
                total += jnp.dot(comb_r[e], back[e, :, cols], preferred_element_type=F32)
            y_v[lax.rem(k, 2), :, pl.ds(i * TN, TN)] = total.astype(BF16)
        y_copy(k).start()

    for r in far_first:
        c_copy(per - 1, chunks - 1, r).start()

    @pl.loop(0, chunks)
    def _(k):
        finish(k)

    for k in (chunks - 2, chunks - 1):
        y_copy(k).wait()
    for k in range(chunks):
        for r in far_first:
            d_copy(1, k, r).wait_send()
    for e in range(per):
        for k in range(chunks):
            for r in far_first:
                c_copy(e, k, r).wait_send()


def solution(mesh):
    n = mesh.shape["ep"]

    def layer(x, expert, slot, gate, w_gate, w_up, w_down):
        per, depth, ff = w_gate.shape
        tokens, top = expert.shape[2:]
        slots = 5 * tokens * top // (4 * per * n)
        rows = n * slots
        chunks = depth // CHUNK
        lo = -(-(ff // TN) // 2) * TN
        any_, vmem = pl.BlockSpec(memory_space=pl.ANY), pl.BlockSpec(memory_space=pltpu.VMEM)
        dma = pltpu.SemaphoreType.DMA
        y = pl.pallas_call(
            functools.partial(kernel, n, slots),
            out_shape=jax.ShapeDtypeStruct((tokens, depth), BF16),
            in_specs=[any_, vmem, vmem, vmem, any_, any_, any_],
            out_specs=any_,
            scratch_shapes=[
                pltpu.VMEM((tokens, depth), BF16),
                pltpu.VMEM((per, rows, depth), BF16),
                pltpu.VMEM((rows - slots, depth), BF16),
                pltpu.VMEM((per, rows - slots, depth), BF16),
                pltpu.VMEM((rows, ff), F32),
                pltpu.VMEM((rows, ff), F32),
                pltpu.VMEM((rows, ff), BF16),
                pltpu.VMEM((KC, lo), BF16),
                pltpu.VMEM((KC, ff - lo), BF16),
                pltpu.VMEM((KC, lo), BF16),
                pltpu.VMEM((KC, ff - lo), BF16),
                pltpu.VMEM((DOWN, ff, NC), BF16),
                pltpu.VMEM((2, tokens, CHUNK), BF16),
                pltpu.VMEM((per, rows, tokens), BF16),
                pltpu.VMEM((per, tokens, slots), BF16),
                pltpu.VMEM((per, tokens, rows - slots), BF16),
                dma((chunks,)), dma((4,)), dma((DOWN,)), dma((2,)),
                dma((chunks, n - 1)), dma((per, chunks, n - 1)),
                dma((per, chunks, n - 1)), dma((per, chunks, n - 1)),
            ],
            compiler_params=pltpu.CompilerParams(
                collective_id=0, has_side_effects=True, vmem_limit_bytes=67_000_000
            ),
            cost_estimate=pl.CostEstimate(
                flops=6 * per * rows * depth * ff, bytes_accessed=6 * per * depth * ff, transcendentals=0
            ),
            name="moe",
        )(
            x.reshape(tokens, depth), expert.reshape(tokens, top), slot.reshape(tokens, top),
            gate.reshape(tokens, top), w_gate, w_up, w_down,
        )
        return y.reshape(x.shape)

    token, weight = P("dp", "ep", None, None), P("ep", None, None)
    return jax.shard_map(
        layer, mesh=mesh, in_specs=(token,) * 4 + (weight,) * 3, out_specs=token, check_vma=False
    )
```

time: 422 us -> 261 us (0.62)
  Pallas kernels: 0 us -> 253 us
  matrix products: 200 us -> 0 us
  blocking collectives: 107 us -> 0 us
  waiting for transfers between devices: 98.8 us -> 0 us
  starting transfers between devices: 5.98 us -> 0 us
    pallas_call x0 -> x1, Pallas kernels: none -> 253 us  [layer(): pl.pallas_call(functools.partial(kernel, n, slots), out_shape=jax.ShapeDt...]
    dot_general x7 -> x0, matrix products: 200 us -> none  [einsum(): return jnp.einsum(form, a.astype(jnp.float32), b.astype(jnp.float32))]
    another operation x1 -> x0, blocking collectives: 107 us -> none  [placed(): return lax.with_sharding_constraint(v, NamedSharding(mesh, P(*spec)))]
    another operation x1 -> x0, waiting for transfers between devices: 98.8 us -> none  [placed(): return lax.with_sharding_constraint(v, NamedSharding(mesh, P(*spec)))]
    another operation x1 -> x0, local copies, waits for them, and re-layouts: 7.74 us -> none  [placed(): return lax.with_sharding_constraint(v, NamedSharding(mesh, P(*spec)))]
    unnamed x12 -> x4, local copies, waits for them, and re-layouts: 1.66 us -> 8.5 us
    another operation x1 -> x0, starting transfers between devices: 5.98 us -> none  [placed(): return lax.with_sharding_constraint(v, NamedSharding(mesh, P(*spec)))]
  transfers between devices with their start and end apart: 1 -> 0, of which waited for: 1 -> 0; matrix products, arithmetic and copies ran while one was open for 1% -> 0% of each run, Pallas kernels for 0% -> 0%
where the time goes in v1:
time: 261 us
  Pallas kernels  253 us (97%)
  local copies, waits for them, and re-layouts  8.5 us (3%)
    pallas_call x1, Pallas kernels, layer(): pl.pallas_call(functools.partial(kernel, n, slots), out_shape=jax.ShapeDt...  253 us
    unnamed x4, local copies, waits for them, and re-layouts  8.5 us

profile of v1, /device:TPU:112, one launch (start us, length us, event | category | flops | bytes accessed | tf_op | source)
XLA Modules:
  0.0 261.1 jit_solution(15105789157236698930)
XLA Ops:
  0.0 1.5 copy.8
  1.5 1.5 copy.9
  2.9 1.5 copy.10
  4.4 252.6 %moe.1 = bf16[256,7168]{1,0:T(8,128)(2,1)} custom-call(bf16[256,7168]{1,0:T(8,128)(2,1)} %bitcast.9, s32[256,2]{1,0:T(8,128)} %bitcast.6, s32[256,2]{1,0:T(8,128)} %bitcast.7, f32[256,2]{1,0:T(8,128)} %bitcast.8, bf16[2,7168,4864]{2,1,0:T(8,128)(2,1)} %wg_hbm.1, bf16[2,7168,4864]{2,1,0:T(8,128)(2,1)} %wu_hbm.1, bf16[2,4864,7168]{2,1,0:T(8,128)(2,1)} %wd_hbm.1), custom_call_target="tpu_custom_call" | custom-call | flops 133882183680 | bytes 418381824 | tf_op jit(solution)/shard_map/moe/pallas_call | solution.py:258
  257.0 4.1 %copy.12 = bf16[1,1,256,7168]{3,2,1,0:T(8,128)(2,1)} copy(bf16[1,1,256,7168]{3,2,1,0:T(8,128)(2,1)} %bitcast.5) | data formatting | bytes 7340032

commit v2 on v0

v2 whole, which is shorter than its diff:
```python
import functools

import jax
import jax.numpy as jnp
from jax import lax
from jax.experimental import pallas as pl
from jax.experimental.pallas import tpu as pltpu
from jax.sharding import PartitionSpec as P

F32, BF16 = jnp.float32, jnp.bfloat16
CHUNK = 1024
TOK = 512
KC = 512
TN = 256
AHEAD = 3


def rows_of_choices(n, per, slots, me, ex, sl):
    owner = lax.shift_right_logical(ex, per.bit_length() - 1)
    place = lax.bitwise_and(owner - me + n, n - 1) * slots + sl
    local = lax.bitwise_and(ex, per - 1)
    return [jnp.where(jnp.logical_and(local == e, sl < slots), place, -1) for e in range(per)]


def spread(row, value, rows, first=0):
    tokens = row.shape[1]
    line = lax.broadcasted_iota(jnp.int32, (rows, tokens), 0) + first
    return sum(jnp.where(line == row[j:j + 1], value[j:j + 1], 0.0) for j in range(row.shape[0]))


def exchange_kernel(
    n, slots, x_hbm, expert_ref, slot_ref, gate_ref, wg_hbm, wu_hbm, wd_hbm, out_hbm, y_hbm, comb_hbm,
    x_v, z, stage, acc, h, w_v, sel, comb,
    x_sem, w_sem, l_sem, y_sem, comb_sem, d_send, d_recv, c_send, c_recv,
):
    per, depth, ff = wg_hbm.shape
    tokens, rows = x_hbm.shape[0], n * slots
    chunks, toks, steps = depth // CHUNK, depth // TOK, depth // KC
    assert TOK == KC and 2 * KC == CHUNK and per == 2
    blocks = [(i, min(CHUNK, ff - i * CHUNK)) for i in range(-(-ff // CHUNK))]
    up_first = len(blocks) * KC
    me = lax.axis_index("ep")

    def peer(r):
        return {"ep": lax.rem(me + r, n)}

    def at(i, size):
        return pl.ds(pl.multiple_of(i * size, size), size)

    def x_copy(e, k):
        b = lax.rem(e * toks + k, 2)
        return pltpu.make_async_copy(x_hbm.at[:, at(k, TOK)], x_v.at[b], x_sem.at[b])

    def buf(e, s):
        return lax.rem(e * (steps + chunks) + s, AHEAD)

    def up_copies(e, s):
        b = buf(e, s)
        return [
            pltpu.make_async_copy(
                w.at[e, at(s, KC), pl.ds(i * CHUNK, width)],
                w_v.at[b, pl.ds(first + i * KC, KC), pl.ds(0, width)], w_sem.at[b],
            )
            for w, first in ((wg_hbm, 0), (wu_hbm, up_first))
            for i, width in blocks
        ]

    def down_copy(e, s):
        b = buf(e, s)
        return pltpu.make_async_copy(
            wd_hbm.at[e, :, at(s - steps, CHUNK)], w_v.at[b, pl.ds(0, ff)], w_sem.at[b]
        )

    def refill(e, s):
        @pl.when(s < steps)
        def _():
            for copy in up_copies(e, s):
                copy.start()

        @pl.when(jnp.logical_and(s >= steps, s < steps + chunks))
        def _():
            down_copy(e, s).start()

        if e + 1 < per:
            @pl.when(s >= steps + chunks)
            def _():
                for copy in up_copies(e + 1, s - steps - chunks):
                    copy.start()

    def await_weights(e, s):
        b = buf(e, s)
        whole = w_v.at[b, pl.ds(0, ff)]
        pltpu.make_async_copy(whole, whole, w_sem.at[b]).wait()

    def d_copy(e, k, r):
        return pltpu.make_async_remote_copy(
            src_ref=stage.at[pl.ds((r - 1) * slots, slots), at(k, TOK)],
            dst_ref=z.at[e, pl.ds(r * slots, slots), at(k, TOK)],
            send_sem=d_send.at[k, r - 1], recv_sem=d_recv.at[e, k, r - 1],
            device_id=peer(r), device_id_type=pl.DeviceIdType.MESH,
        )

    def c_copy(e, k, r):
        return pltpu.make_async_remote_copy(
            src_ref=z.at[e, pl.ds(r * slots, slots), at(k, CHUNK)],
            dst_ref=out_hbm.at[e, pl.ds(r * slots, slots), at(k, CHUNK)],
            send_sem=c_send.at[e, k, r - 1], recv_sem=c_recv.at[e, k, r - 1],
            device_id=peer(n - r), device_id_type=pl.DeviceIdType.MESH,
        )

    def l_copy(e, k):
        here = (e, pl.ds(0, slots), at(k, CHUNK))
        return pltpu.make_async_copy(z.at[here], out_hbm.at[here], l_sem.at[e, k])

    far_first = (2, 1, 3)

    for k in range(2):
        x_copy(0, k).start()
    for v in range(AHEAD):
        for copy in up_copies(0, v):
            copy.start()
    barrier = pltpu.get_barrier_semaphore()
    for r in range(1, n):
        pl.semaphore_signal(barrier, inc=1, device_id=peer(r), device_id_type=pl.DeviceIdType.MESH)

    choice_rows = rows_of_choices(n, per, slots, me, expert_ref[...], slot_ref[...])

    def select(e):
        row = choice_rows[e]

        @pl.loop(0, n)
        def _(r):
            sel[e, at(r, slots)] = spread(row, jnp.ones(row.shape, F32), slots, r * slots).astype(BF16)

    select(0)

    def gather(e, k):
        x_copy(e, k).wait()
        b = lax.rem(e * toks + k, 2)
        for i in range(TOK // TN):
            cols = pl.ds(pl.multiple_of(k * TOK + i * TN, TN), TN)
            some = jnp.dot(sel[e], x_v[b, :, pl.ds(i * TN, TN)], preferred_element_type=F32).astype(BF16)
            z[e, :slots, cols] = some[:slots]
            stage[:, cols] = some[slots:]

        @pl.when(k + 2 < toks)
        def _():
            x_copy(e, k + 2).start()

        if e == 0:
            @pl.when(k + 2 >= toks)
            def _():
                x_copy(1, k + 2 - toks).start()

    def send(e, k):
        for r in far_first:
            d_copy(e, k, r).start()

    def give(e, k):
        for r in far_first:
            c_copy(e, k, r).start()
        l_copy(e, k).start()

    pl.semaphore_wait(barrier, n - 1)
    gather(0, 0)
    select(1)
    send(0, 0)

    @pl.loop(1, toks)
    def _(k):
        gather(0, k)

        @pl.when(k > 1)
        def _():
            send(0, k - 1)

    @pl.loop(0, ff // TN)
    def _(i):
        for j in range(2):
            acc[j, :, at(i, TN)] = jnp.zeros((rows, TN), F32)

    send(0, toks - 1)

    gates = gate_ref[...].astype(BF16).astype(F32)
    for e, row in enumerate(choice_rows):
        comb[e] = spread(row, gates, rows).T.astype(BF16)
    comb_copy = pltpu.make_async_copy(comb, comb_hbm, comb_sem)

    def again(k):
        for r in far_first:
            d_copy(0, k, r).wait_send()
        gather(1, k)

    def arrive(e, s):
        for r in far_first:
            d_copy(e, s, r).wait_recv()

    await_weights(0, 0)
    for e in range(per):
        def project(s, i, j):
            block, off = i * TN // CHUNK, i * TN % CHUNK
            return acc[j, :, pl.ds(i * TN, TN)] + jnp.dot(
                z[e, :, at(s, KC)], w_v[buf(e, s), pl.ds(j * up_first + block * KC, KC), pl.ds(off, TN)],
                preferred_element_type=F32,
            )

        @pl.loop(0, steps - 1)
        def _(s):
            arrive(e, s)
            if e == 0:
                @pl.when(s >= 1)
                def _():
                    again(s - 1)
            for i in range(ff // TN):
                for j in range(2):
                    acc[j, :, pl.ds(i * TN, TN)] = project(s, i, j)
            refill(e, s + AHEAD)
            await_weights(e, s + 1)
            if e == 0:
                @pl.when(s >= 1)
                def _():
                    send(1, s - 1)

        arrive(e, steps - 1)
        if e == 0:
            again(toks - 2)
        for i in range(ff // TN):
            gate, up = project(steps - 1, i, 0), project(steps - 1, i, 1)
            h[:, pl.ds(i * TN, TN)] = (jax.nn.silu(gate) * up).astype(BF16)
            for j in range(2):
                if e + 1 < per:
                    acc[j, :, pl.ds(i * TN, TN)] = jnp.zeros((rows, TN), F32)
        refill(e, jnp.int32(steps - 1 + AHEAD))
        await_weights(e, steps)
        if e == 0:
            again(toks - 1)
            send(1, toks - 2)
            send(1, toks - 1)

        @pl.loop(0, chunks)
        def _(p):
            s = steps + p
            for i in range(CHUNK // TN):
                some = jnp.dot(h[...], w_v[buf(e, s), pl.ds(0, ff), pl.ds(i * TN, TN)], preferred_element_type=F32)
                z[e, :, pl.ds(pl.multiple_of(p * CHUNK + i * TN, TN), TN)] = some.astype(BF16)
            refill(e, s + AHEAD)
            if e + 1 < per:
                await_weights(e, s + 1)
            else:
                @pl.when(p + 1 < chunks)
                def _():
                    await_weights(e, s + 1)
            give(e, p)

    comb_copy.start()

    def y_copy(k):
        b = lax.rem(k, AHEAD)
        return pltpu.make_async_copy(
            w_v.at[b, pl.ds(per * rows, tokens)], y_hbm.at[:, at(k, CHUNK)], y_sem.at[b]
        )

    def back_copy(e, k):
        b = lax.rem(k, AHEAD)
        return pltpu.make_async_copy(
            out_hbm.at[e, :, at(k, CHUNK)], w_v.at[b, pl.ds(e * rows, rows)], y_sem.at[b]
        )

    def all_back(k):
        for e in range(per):
            l_copy(e, k).wait()
            for r in far_first:
                c_copy(e, k, r).wait_recv()

    @pl.loop(0, chunks - 1)
    def _(k):
        b = lax.rem(k, AHEAD)
        all_back(k)

        @pl.when(k >= AHEAD)
        def _():
            y_copy(k - AHEAD).wait()
        for e in range(per):
            back_copy(e, k).start()
        for e in range(per):
            back_copy(e, k).wait()
        for i in range(CHUNK // TN):
            cols = pl.ds(i * TN, TN)
            total = 0.0
            for e in range(per):
                total += jnp.dot(comb[e], w_v[b, pl.ds(e * rows, rows), cols], preferred_element_type=F32)
            w_v[b, pl.ds(per * rows, tokens), cols] = total.astype(BF16)
        y_copy(k).start()

    for k in range(chunks - 1 - AHEAD, chunks - 1):
        y_copy(k).wait()
    comb_copy.wait()

    @pl.loop(0, toks)
    def _(k):
        for r in far_first:
            d_copy(1, k, r).wait_send()

    @pl.loop(0, chunks)
    def _(k):
        for e in range(per):
            for r in far_first:
                c_copy(e, k, r).wait_send()

    all_back(chunks - 1)


def last_kernel(comb_hbm, rows_hbm, y_in_hbm, y_hbm, comb, rows_v, y_v, in_sem, out_sem):
    per, _, depth = rows_hbm.shape
    chunks = depth // CHUNK
    last = chunks - 1

    def in_copy(k):
        cols = pl.ds(k * CHUNK, CHUNK)
        if k == last:
            return pltpu.make_async_copy(rows_hbm.at[:, :, cols], rows_v, in_sem.at[k])
        return pltpu.make_async_copy(y_in_hbm.at[:, cols], y_v.at[:, cols], in_sem.at[k])

    def out_copy(k):
        cols = pl.ds(k * CHUNK, CHUNK)
        return pltpu.make_async_copy(y_v.at[:, cols], y_hbm.at[:, cols], out_sem.at[k])

    comb_copy = pltpu.make_async_copy(comb_hbm, comb, in_sem.at[chunks])
    comb_copy.start()
    in_copy(last).start()
    for k in range(last):
        in_copy(k).start()
    comb_copy.wait()
    in_copy(last).wait()
    for i in range(CHUNK // TN):
        cols = pl.ds(i * TN, TN)
        total = 0.0
        for e in range(per):
            total += jnp.dot(comb[e], rows_v[e, :, cols], preferred_element_type=F32)
        y_v[:, pl.ds(last * CHUNK + i * TN, TN)] = total.astype(BF16)
    out_copy(last).start()
    for k in range(last):
        in_copy(k).wait()
        out_copy(k).start()
    for k in range(chunks):
        out_copy(k).wait()


def solution(mesh):
    n = mesh.shape["ep"]

    def layer(x, expert, slot, gate, w_gate, w_up, w_down):
        per, depth, ff = w_gate.shape
        tokens, top = expert.shape[2:]
        slots = 5 * tokens * top // (4 * per * n)
        rows, chunks, toks = n * slots, depth // CHUNK, depth // TOK
        any_, vmem = pl.BlockSpec(memory_space=pl.ANY), pl.BlockSpec(memory_space=pltpu.VMEM)
        dma = pltpu.SemaphoreType.DMA
        expert, slot, gate = (a.reshape(tokens, top).T for a in (expert, slot, gate))
        results, sums, comb = pl.pallas_call(
            functools.partial(exchange_kernel, n, slots),
            out_shape=[
                jax.ShapeDtypeStruct((per, rows, depth), BF16),
                jax.ShapeDtypeStruct((tokens, depth), BF16),
                jax.ShapeDtypeStruct((per, tokens, rows), BF16),
            ],
            in_specs=[any_, vmem, vmem, vmem, any_, any_, any_],
            out_specs=[any_, any_, any_],
            scratch_shapes=[
                pltpu.VMEM((2, tokens, TOK), BF16),
                pltpu.VMEM((per, rows, depth), BF16),
                pltpu.VMEM((rows - slots, depth), BF16),
                pltpu.VMEM((2, rows, ff), F32),
                pltpu.VMEM((rows, ff), BF16),
                pltpu.VMEM((AHEAD, 2 * KC * -(-ff // CHUNK), CHUNK), BF16),
                pltpu.VMEM((per, rows, tokens), BF16),
                pltpu.VMEM((per, tokens, rows), BF16),
                dma((2,)), dma((AHEAD,)), dma((per, chunks)), dma((AHEAD,)), dma(()),
                dma((toks, n - 1)), dma((per, toks, n - 1)),
                dma((per, chunks, n - 1)), dma((per, chunks, n - 1)),
            ],
            compiler_params=pltpu.CompilerParams(
                collective_id=0, has_side_effects=True, vmem_limit_bytes=67_000_000
            ),
            cost_estimate=pl.CostEstimate(
                flops=6 * per * rows * depth * ff, bytes_accessed=6 * per * depth * ff, transcendentals=0
            ),
            name="exchange",
        )(x.reshape(tokens, depth), expert, slot, gate, w_gate, w_up, w_down)
        y = pl.pallas_call(
            last_kernel,
            out_shape=jax.ShapeDtypeStruct((tokens, depth), BF16),
            in_specs=[any_, any_, any_],
            out_specs=any_,
            scratch_shapes=[
                pltpu.VMEM((per, tokens, rows), BF16),
                pltpu.VMEM((per, rows, CHUNK), BF16),
                pltpu.VMEM((tokens, depth), BF16),
                dma((chunks + 1,)), dma((chunks,)),
            ],
            compiler_params=pltpu.CompilerParams(vmem_limit_bytes=60_000_000),
            name="last",
        )(comb, results, sums)
        return y.reshape(x.shape)

    token, weight = P("dp", "ep", None, None), P("ep", None, None)
    return jax.shard_map(
        layer, mesh=mesh, in_specs=(token,) * 4 + (weight,) * 3, out_specs=token, check_vma=False
    )
```

time: 422 us -> 218 us (0.52)
  Pallas kernels: 0 us -> 218 us
  matrix products: 200 us -> 0 us
  blocking collectives: 107 us -> 0 us
  waiting for transfers between devices: 98.8 us -> 0 us
  local copies, waits for them, and re-layouts: 9.55 us -> 0 us
  starting transfers between devices: 5.98 us -> 0 us
    pallas_call x0 -> x2, Pallas kernels: none -> 218 us  [the longest x1 213 us: layer(): pl.pallas_call(functools.partial(exchange_kernel, n, slots), out_shape=[j...]
    dot_general x7 -> x0, matrix products: 200 us -> none  [einsum(): return jnp.einsum(form, a.astype(jnp.float32), b.astype(jnp.float32))]
    another operation x1 -> x0, blocking collectives: 107 us -> none  [placed(): return lax.with_sharding_constraint(v, NamedSharding(mesh, P(*spec)))]
    another operation x1 -> x0, waiting for transfers between devices: 98.8 us -> none  [placed(): return lax.with_sharding_constraint(v, NamedSharding(mesh, P(*spec)))]
    another operation x1 -> x0, local copies, waits for them, and re-layouts: 7.74 us -> none  [placed(): return lax.with_sharding_constraint(v, NamedSharding(mesh, P(*spec)))]
    another operation x1 -> x0, starting transfers between devices: 5.98 us -> none  [placed(): return lax.with_sharding_constraint(v, NamedSharding(mesh, P(*spec)))]
  transfers between devices with their start and end apart: 1 -> 0, of which waited for: 1 -> 0; matrix products, arithmetic and copies ran while one was open for 1% -> 0% of each run, Pallas kernels for 0% -> 0%
where the time goes in v2:
time: 218 us
  Pallas kernels  218 us (100%)
    pallas_call x1, Pallas kernels, layer(): pl.pallas_call(functools.partial(exchange_kernel, n, slots), out_shape=[j...  213 us

profile of v2, /device:TPU:112, one launch (start us, length us, event | category | flops | bytes accessed | tf_op | source)
XLA Modules:
  0.0 217.7 jit_solution(12716399348320140955)
XLA Ops:
  0.0 213.5 %exchange.1 = (bf16[2,320,7168]{2,1,0:T(8,128)(2,1)}, bf16[256,7168]{1,0:T(8,128)(2,1)}, bf16[2,256,320]{2,1,0:T(8,128)(2,1)}) custom-call(bf16[256,7168]{1,0:T(8,128)(2,1)} %bitcast.11, s32[2,256]{1,0:T(2,128)} %bitcast.12, s32[2,256]{1,0:T(2,128)} %bitcast.13, f32[2,256]{1,0:T(2,128)} %bitcast.14, bf16[2,7168,4864]{2,1,0:T(8,128)(2,1)} %wg_hbm.1, ...), custom_call_target="tpu_custom_call" | custom-call | flops 133882183680 | bytes 418381824 | tf_op jit(solution)/shard_map/exchange/pallas_call | solution.py:360
  213.5 4.1 %last.1 = bf16[256,7168]{1,0:T(8,128)(2,1)} custom-call(bf16[2,256,320]{2,1,0:T(8,128)(2,1)} %get-tuple-element.8.comb_hbm, bf16[2,320,7168]{2,1,0:T(8,128)(2,1)} %get-tuple-element.9.rows_hbm, bf16[256,7168]{1,0:T(8,128)(2,1)} %get-tuple-element.10.y_in_hbm), custom_call_target="tpu_custom_call" | custom-call | tf_op jit(solution)/shard_map/last/pallas_call | solution.py:390

commit v3 on v2

--- a/solution.py
+++ b/solution.py
@@ -12,7 +12,7 @@
 TOK = 512
 KC = 512
 TN = 256
-AHEAD = 3
+AHEAD = 2
 
 
 def rows_of_choices(n, per, slots, me, ex, sl):
@@ -29,14 +29,15 @@
 
 
 def exchange_kernel(
-    n, slots, x_hbm, expert_ref, slot_ref, gate_ref, wg_hbm, wu_hbm, wd_hbm, out_hbm, y_hbm, comb_hbm,
-    x_v, z, stage, acc, h, w_v, sel, comb,
-    x_sem, w_sem, l_sem, y_sem, comb_sem, d_send, d_recv, c_send, c_recv,
+    n, slots, x_hbm, expert_ref, slot_ref, gate_ref, wg_hbm, wu_hbm, wd_hbm, y_hbm,
+    x_v, z, stage, back, acc, h, w_v, sel, comb_l, comb_r,
+    x_sem, w_sem, y_sem, d_send, d_recv, c_send, c_recv,
 ):
     per, depth, ff = wg_hbm.shape
     tokens, rows = x_hbm.shape[0], n * slots
     chunks, toks, steps = depth // CHUNK, depth // TOK, depth // KC
-    assert TOK == KC and 2 * KC == CHUNK and per == 2
+    per_chunk = CHUNK // KC
+    assert TOK == KC and steps % per_chunk == 0 and per_chunk == 2 and per == 2
     blocks = [(i, min(CHUNK, ff - i * CHUNK)) for i in range(-(-ff // CHUNK))]
     up_first = len(blocks) * KC
     me = lax.axis_index("ep")
@@ -94,8 +95,8 @@
 
     def d_copy(e, k, r):
         return pltpu.make_async_remote_copy(
-            src_ref=stage.at[pl.ds((r - 1) * slots, slots), at(k, TOK)],
-            dst_ref=z.at[e, pl.ds(r * slots, slots), at(k, TOK)],
+            src_ref=stage.at[pl.ds((r - 1) * slots, slots), at(k, CHUNK)],
+            dst_ref=z.at[e, pl.ds(r * slots, slots), at(k, CHUNK)],
             send_sem=d_send.at[k, r - 1], recv_sem=d_recv.at[e, k, r - 1],
             device_id=peer(r), device_id_type=pl.DeviceIdType.MESH,
         )
@@ -103,14 +104,10 @@
     def c_copy(e, k, r):
         return pltpu.make_async_remote_copy(
             src_ref=z.at[e, pl.ds(r * slots, slots), at(k, CHUNK)],
-            dst_ref=out_hbm.at[e, pl.ds(r * slots, slots), at(k, CHUNK)],
+            dst_ref=back.at[e, pl.ds((r - 1) * slots, slots), at(k, CHUNK)],
             send_sem=c_send.at[e, k, r - 1], recv_sem=c_recv.at[e, k, r - 1],
             device_id=peer(n - r), device_id_type=pl.DeviceIdType.MESH,
         )
-
-    def l_copy(e, k):
-        here = (e, pl.ds(0, slots), at(k, CHUNK))
-        return pltpu.make_async_copy(z.at[here], out_hbm.at[here], l_sem.at[e, k])
 
     far_first = (2, 1, 3)
 
@@ -159,16 +156,19 @@
     def give(e, k):
         for r in far_first:
             c_copy(e, k, r).start()
-        l_copy(e, k).start()
 
     pl.semaphore_wait(barrier, n - 1)
-    gather(0, 0)
+    def gathers(e, k):
+        for i in range(per_chunk):
+            gather(e, per_chunk * k + i)
+
+    gathers(0, 0)
     select(1)
     send(0, 0)
 
-    @pl.loop(1, toks)
+    @pl.loop(1, chunks)
     def _(k):
-        gather(0, k)
+        gathers(0, k)
 
         @pl.when(k > 1)
         def _():
@@ -179,17 +179,17 @@
         for j in range(2):
             acc[j, :, at(i, TN)] = jnp.zeros((rows, TN), F32)
 
-    send(0, toks - 1)
+    send(0, chunks - 1)
 
     gates = gate_ref[...].astype(BF16).astype(F32)
     for e, row in enumerate(choice_rows):
-        comb[e] = spread(row, gates, rows).T.astype(BF16)
-    comb_copy = pltpu.make_async_copy(comb, comb_hbm, comb_sem)
+        comb_l[e] = spread(row, gates, slots).T.astype(BF16)
+        comb_r[e] = spread(row, gates, rows - slots, slots).T.astype(BF16)
 
     def again(k):
         for r in far_first:
             d_copy(0, k, r).wait_send()
-        gather(1, k)
+        gathers(1, k)
 
     def arrive(e, s):
         for r in far_first:
@@ -206,24 +206,25 @@
 
         @pl.loop(0, steps - 1)
         def _(s):
-            arrive(e, s)
-            if e == 0:
-                @pl.when(s >= 1)
-                def _():
-                    again(s - 1)
+            k = lax.div(s, per_chunk)
+
+            @pl.when(lax.rem(s, per_chunk) == 0)
+            def _():
+                arrive(e, k)
+                if e == 0:
+                    @pl.when(s > 0)
+                    def _():
+                        again(k - 1)
             for i in range(ff // TN):
                 for j in range(2):
                     acc[j, :, pl.ds(i * TN, TN)] = project(s, i, j)
             refill(e, s + AHEAD)
             await_weights(e, s + 1)
             if e == 0:
-                @pl.when(s >= 1)
+                @pl.when(jnp.logical_and(lax.rem(s, per_chunk) == 0, s > 0))
                 def _():
-                    send(1, s - 1)
-
-        arrive(e, steps - 1)
-        if e == 0:
-            again(toks - 2)
+                    send(1, k - 1)
+
         for i in range(ff // TN):
             gate, up = project(steps - 1, i, 0), project(steps - 1, i, 1)
             h[:, pl.ds(i * TN, TN)] = (jax.nn.silu(gate) * up).astype(BF16)
@@ -233,9 +234,8 @@
         refill(e, jnp.int32(steps - 1 + AHEAD))
         await_weights(e, steps)
         if e == 0:
-            again(toks - 1)
-            send(1, toks - 2)
-            send(1, toks - 1)
+            again(chunks - 1)
+            send(1, chunks - 1)
 
         @pl.loop(0, chunks)
         def _(p):
@@ -252,94 +252,55 @@
                     await_weights(e, s + 1)
             give(e, p)
 
-    comb_copy.start()
-
     def y_copy(k):
         b = lax.rem(k, AHEAD)
-        return pltpu.make_async_copy(
-            w_v.at[b, pl.ds(per * rows, tokens)], y_hbm.at[:, at(k, CHUNK)], y_sem.at[b]
-        )
-
-    def back_copy(e, k):
+        return pltpu.make_async_copy(w_v.at[b, pl.ds(0, tokens)], y_hbm.at[:, at(k, CHUNK)], y_sem.at[b])
+
+    @pl.loop(0, chunks)
+    def _(k):
         b = lax.rem(k, AHEAD)
-        return pltpu.make_async_copy(
-            out_hbm.at[e, :, at(k, CHUNK)], w_v.at[b, pl.ds(e * rows, rows)], y_sem.at[b]
-        )
-
-    def all_back(k):
         for e in range(per):
-            l_copy(e, k).wait()
             for r in far_first:
                 c_copy(e, k, r).wait_recv()
 
-    @pl.loop(0, chunks - 1)
-    def _(k):
-        b = lax.rem(k, AHEAD)
-        all_back(k)
-
         @pl.when(k >= AHEAD)
         def _():
             y_copy(k - AHEAD).wait()
-        for e in range(per):
-            back_copy(e, k).start()
-        for e in range(per):
-            back_copy(e, k).wait()
         for i in range(CHUNK // TN):
-            cols = pl.ds(i * TN, TN)
+            cols = pl.ds(pl.multiple_of(k * CHUNK + i * TN, TN), TN)
             total = 0.0
             for e in range(per):
-                total += jnp.dot(comb[e], w_v[b, pl.ds(e * rows, rows), cols], preferred_element_type=F32)
-            w_v[b, pl.ds(per * rows, tokens), cols] = total.astype(BF16)
+                total += jnp.dot(comb_l[e], z[e, :slots, cols], preferred_element_type=F32)
+                total += jnp.dot(comb_r[e], back[e, :, cols], preferred_element_type=F32)
+            w_v[b, :tokens, pl.ds(i * TN, TN)] = total.astype(BF16)
         y_copy(k).start()
 
-    for k in range(chunks - 1 - AHEAD, chunks - 1):
+    for k in range(chunks - AHEAD, chunks):
         y_copy(k).wait()
-    comb_copy.wait()
-
-    @pl.loop(0, toks)
-    def _(k):
-        for r in far_first:
-            d_copy(1, k, r).wait_send()
 
     @pl.loop(0, chunks)
     def _(k):
+        for r in far_first:
+            d_copy(1, k, r).wait_send()
         for e in range(per):
             for r in far_first:
                 c_copy(e, k, r).wait_send()
 
-    all_back(chunks - 1)
-
-
-def last_kernel(comb_hbm, rows_hbm, y_in_hbm, y_hbm, comb, rows_v, y_v, in_sem, out_sem):
-    per, _, depth = rows_hbm.shape
-    chunks = depth // CHUNK
-    last = chunks - 1
+
+def copy_kernel(y_in_hbm, y_hbm, y_v, in_sem, out_sem):
+    chunks = y_v.shape[1] // CHUNK
 
     def in_copy(k):
         cols = pl.ds(k * CHUNK, CHUNK)
-        if k == last:
-            return pltpu.make_async_copy(rows_hbm.at[:, :, cols], rows_v, in_sem.at[k])
         return pltpu.make_async_copy(y_in_hbm.at[:, cols], y_v.at[:, cols], in_sem.at[k])
 
     def out_copy(k):
         cols = pl.ds(k * CHUNK, CHUNK)
         return pltpu.make_async_copy(y_v.at[:, cols], y_hbm.at[:, cols], out_sem.at[k])
 
-    comb_copy = pltpu.make_async_copy(comb_hbm, comb, in_sem.at[chunks])
-    comb_copy.start()
-    in_copy(last).start()
-    for k in range(last):
+    for k in range(chunks):
         in_copy(k).start()
-    comb_copy.wait()
-    in_copy(last).wait()
-    for i in range(CHUNK // TN):
-        cols = pl.ds(i * TN, TN)
-        total = 0.0
-        for e in range(per):
-            total += jnp.dot(comb[e], rows_v[e, :, cols], preferred_element_type=F32)
-        y_v[:, pl.ds(last * CHUNK + i * TN, TN)] = total.astype(BF16)
-    out_copy(last).start()
-    for k in range(last):
+    for k in range(chunks):
         in_copy(k).wait()
         out_copy(k).start()
     for k in range(chunks):
@@ -353,30 +314,28 @@
         per, depth, ff = w_gate.shape
         tokens, top = expert.shape[2:]
         slots = 5 * tokens * top // (4 * per * n)
-        rows, chunks, toks = n * slots, depth // CHUNK, depth // TOK
+        rows, chunks = n * slots, depth // CHUNK
         any_, vmem = pl.BlockSpec(memory_space=pl.ANY), pl.BlockSpec(memory_space=pltpu.VMEM)
         dma = pltpu.SemaphoreType.DMA
         expert, slot, gate = (a.reshape(tokens, top).T for a in (expert, slot, gate))
-        results, sums, comb = pl.pallas_call(
+        sums = pl.pallas_call(
             functools.partial(exchange_kernel, n, slots),
-            out_shape=[
-                jax.ShapeDtypeStruct((per, rows, depth), BF16),
-                jax.ShapeDtypeStruct((tokens, depth), BF16),
-                jax.ShapeDtypeStruct((per, tokens, rows), BF16),
-            ],
+            out_shape=jax.ShapeDtypeStruct((tokens, depth), BF16),
             in_specs=[any_, vmem, vmem, vmem, any_, any_, any_],
-            out_specs=[any_, any_, any_],
+            out_specs=any_,
             scratch_shapes=[
                 pltpu.VMEM((2, tokens, TOK), BF16),
                 pltpu.VMEM((per, rows, depth), BF16),
                 pltpu.VMEM((rows - slots, depth), BF16),
+                pltpu.VMEM((per, rows - slots, depth), BF16),
                 pltpu.VMEM((2, rows, ff), F32),
                 pltpu.VMEM((rows, ff), BF16),
                 pltpu.VMEM((AHEAD, 2 * KC * -(-ff // CHUNK), CHUNK), BF16),
                 pltpu.VMEM((per, rows, tokens), BF16),
-                pltpu.VMEM((per, tokens, rows), BF16),
-                dma((2,)), dma((AHEAD,)), dma((per, chunks)), dma((AHEAD,)), dma(()),
-                dma((toks, n - 1)), dma((per, toks, n - 1)),
+                pltpu.VMEM((per, tokens, slots), BF16),
+                pltpu.VMEM((per, tokens, rows - slots), BF16),
+                dma((2,)), dma((AHEAD,)), dma((AHEAD,)),
+                dma((chunks, n - 1)), dma((per, chunks, n - 1)),
                 dma((per, chunks, n - 1)), dma((per, chunks, n - 1)),
             ],
             compiler_params=pltpu.CompilerParams(
@@ -388,19 +347,14 @@
             name="exchange",
         )(x.reshape(tokens, depth), expert, slot, gate, w_gate, w_up, w_down)
         y = pl.pallas_call(
-            last_kernel,
+            copy_kernel,
             out_shape=jax.ShapeDtypeStruct((tokens, depth), BF16),
-            in_specs=[any_, any_, any_],
+            in_specs=[any_],
             out_specs=any_,
-            scratch_shapes=[
-                pltpu.VMEM((per, tokens, rows), BF16),
-                pltpu.VMEM((per, rows, CHUNK), BF16),
-                pltpu.VMEM((tokens, depth), BF16),
-                dma((chunks + 1,)), dma((chunks,)),
-            ],
+            scratch_shapes=[pltpu.VMEM((tokens, depth), BF16), dma((chunks,)), dma((chunks,))],
             compiler_params=pltpu.CompilerParams(vmem_limit_bytes=60_000_000),
-            name="last",
-        )(comb, results, sums)
+            name="copy",
+        )(sums)
         return y.reshape(x.shape)
 
     token, weight = P("dp", "ep", None, None), P("ep", None, None)

time: 218 us -> 216 us (level)
  Pallas kernels: 218 us -> 215 us
    pallas_call x2, Pallas kernels: 218 us -> 215 us  [the longest x1 212 us: layer(): pl.pallas_call(functools.partial(exchange_kernel, n, slots), out_shape=ja...]
where the time goes in v3:
time: 216 us; the launch traced here: 215 us
  Pallas kernels  215 us (100%)
    pallas_call x1, Pallas kernels, layer(): pl.pallas_call(functools.partial(exchange_kernel, n, slots), out_shape=ja...  212 us

profile of v3, /device:TPU:112, one launch (start us, length us, event | category | flops | bytes accessed | tf_op | source)
XLA Modules:
  0.0 215.0 jit_solution(14049524572483269209)
XLA Ops:
  0.0 211.8 %exchange.1.y_in_hbm = bf16[256,7168]{1,0:T(8,128)(2,1)} custom-call(bf16[256,7168]{1,0:T(8,128)(2,1)} %bitcast.11, s32[2,256]{1,0:T(2,128)} %bitcast.12, s32[2,256]{1,0:T(2,128)} %bitcast.13, f32[2,256]{1,0:T(2,128)} %bitcast.14, bf16[2,7168,4864]{2,1,0:T(8,128)(2,1)} %wg_hbm.1, bf16[2,7168,4864]{2,1,0:T(8,128)(2,1)} %wu_hbm.1, bf16[2,4864,7168]{2,1,0:T(8,128)(2,1)} %wd_hbm.1), custom_call_target="tpu_custom_call" | custom-call | flops 133882183680 | bytes 418381824 | tf_op jit(solution)/shard_map/exchange/pallas_call | solution.py:321
  211.8 3.1 %copy.9 = bf16[256,7168]{1,0:T(8,128)(2,1)} custom-call(bf16[256,7168]{1,0:T(8,128)(2,1)} %exchange.1.y_in_hbm), custom_call_target="tpu_custom_call" | custom-call | tf_op jit(solution)/shard_map/copy/pallas_call | solution.py:349
